TPU v7x, 256 devices: a whole 4x4x8 slice. The times are simulated.
256 devices in a mesh: rep: 2 (over core), dp: 128 (over x, y, z).
Axes of the slice: x: 4, y: 4, z: 8, core: 2. Of those that a mesh axis runs over, the one named last changes fastest.
Arguments:
- x: bfloat16 [256, 2048, 1024], P(('rep', 'dp')), parts along dimension 0
- dy: bfloat16 [256, 2048, 1024], P(('rep', 'dp')), parts along dimension 0
- w_gate: bfloat16 [2, 1024, 3584], P(None, 'dp')
- w_up: bfloat16 [2, 1024, 3584], P(None, 'dp')
- w_down: bfloat16 [2, 3584, 1024], P(None, 'dp')
Outputs:
- output 1: bfloat16 [256, 2048, 1024], P(('rep', 'dp')), parts along dimension 0
- output 2: bfloat16 [4, 1024, 3584], P('rep', 'dp'), parts along dimension 0
- output 3: bfloat16 [4, 1024, 3584], P('rep', 'dp'), parts along dimension 0
- output 4: bfloat16 [4, 3584, 1024], P('rep', 'dp'), parts along dimension 0
There are 2 independent parts. A program takes and returns all parts, laid end to end along the dimension named above; an argument that names none is the same for every part.
All inputs are finite; a program needn't handle non-finite values.
Results may differ from a plain program's by a relative error of at most 0.018.
Values are sent between devices in bfloat16 or wider.
A program may use at most 768 MiB of HBM per device.

v0:
```python
import jax
import jax.numpy as jnp
from jax import lax

NAMES = ("w_gate", "w_up", "w_down")


def matmul(a, w):
    return jnp.dot(a, w, preferred_element_type=jnp.float32).astype(jnp.bfloat16)


def normed(h):
    wide = h.astype(jnp.float32)
    scale = lax.rsqrt(jnp.mean(wide**2, -1, keepdims=True) + 1e-6)
    return (wide * scale).astype(jnp.bfloat16)


def layer(h, w):
    a = normed(h)
    gate = jnp.dot(a, w["w_gate"], preferred_element_type=jnp.float32)
    up = jnp.dot(a, w["w_up"], preferred_element_type=jnp.float32)
    return h + matmul((jax.nn.silu(gate) * up).astype(jnp.bfloat16), w["w_down"])


def stack(weights, h):
    for number in range(weights["w_gate"].shape[0]):
        h = layer(h, {name: w[number] for name, w in weights.items()})
    return h


def solution(mesh):
    groups = mesh.shape["rep"]

    def step(x, dy, *weights):
        shape = x.shape
        x, dy = (t.reshape(groups, -1, *t.shape[1:]) for t in (x, dy))

        def of_a_group(x, dy):
            _, back = jax.vjp(stack, dict(zip(NAMES, weights, strict=True)), x)
            by_weights, by_x = back(dy)
            return (by_x, *(by_weights[name] for name in NAMES))

        by_x, *by_weights = jax.vmap(of_a_group)(x, dy)
        return (by_x.reshape(shape), *(t.reshape(-1, *t.shape[2:]) for t in by_weights))

    return step
```

profile of v0, /device:TPU:64, one launch (start us, length us, event | category | flops | bytes accessed | tf_op | source)
XLA Modules:
  0.0 3724.7 jit_solution(13520091601513771497)
XLA Ops:
  7.2 1.5 fusion.111
  8.8 1.5 fusion.110
  10.4 1.9 fusion.112
  14.1 3.1 fusion.43
  17.1 6.4 copy.11
  24.2 6.5 copy.10
  30.7 103.7 %all-gather.29.cloned.1.call-done = bf16[1,1024,3584]{2,1,0:T(8,128)(2,1)} async-done(((bf16[1,8,3584]{2,1,0:T(8,128)(2,1)}), bf16[1,1024,3584]{2,1,0:T(8,128)(2,1)}) %all-gather.29.cloned.1.call-update) | async-done | bytes 7340048 | tf_op jit(solution)/vmap(jvp())/squeeze | solution.py:27
  134.3 23.5 fusion.71
  157.8 98.8 %all-gather.31.cloned.1.call-done = bf16[1,1024,3584]{2,1,0:T(8,128)(2,1)} async-done(((bf16[1,8,3584]{2,1,0:T(8,128)(2,1)}), bf16[1,1024,3584]{2,1,0:T(8,128)(2,1)}) %all-gather.31.cloned.1.call-update) | async-done | bytes 7340048 | tf_op jit(solution)/vmap(jvp())/squeeze | solution.py:27
  256.6 23.4 fusion.67
  280.1 25.8 fusion.26
  305.9 94.5 %all-gather.33.cloned.1.call-done = bf16[1,3584,1024]{2,0,1:T(2,128)(2,1)} async-done(((bf16[1,28,1024]{2,0,1:T(2,128)(2,1)}), bf16[1,3584,1024]{2,0,1:T(2,128)(2,1)}) %all-gather.33.cloned.1.call-update) | async-done | bytes 7340048 | tf_op jit(solution)/vmap(jvp())/squeeze | solution.py:27
  400.3 24.4 fusion.51
  425.4 118.8 %all-gather.37.cloned.1.call-done = bf16[1,3584,1024]{2,0,1:T(2,128)(2,1)} async-done(((bf16[1,28,1024]{2,0,1:T(2,128)(2,1)}), bf16[1,3584,1024]{2,0,1:T(2,128)(2,1)}) %all-gather.37.cloned.1.call-update) | async-done | bytes 7340048 | tf_op jit(solution)/vmap(jvp())/squeeze | solution.py:27
  544.3 23.3 convolution_convert_fusion.1
  567.6 99.2 %all-gather.35.cloned.1.call-done = bf16[1,1024,3584]{2,1,0:T(8,128)(2,1)} async-done(((bf16[1,8,3584]{2,1,0:T(8,128)(2,1)}), bf16[1,1024,3584]{2,1,0:T(8,128)(2,1)}) %all-gather.35.cloned.1.call-update) | async-done | bytes 7340048 | tf_op jit(solution)/vmap(jvp())/squeeze | solution.py:27
  666.7 24.8 fusion.64
  691.5 27.1 fusion.37
  718.7 70.8 %all-gather.39.cloned.1.call-done = bf16[1,1024,3584]{2,1,0:T(8,128)(2,1)} async-done(((bf16[1,8,3584]{2,1,0:T(8,128)(2,1)}), bf16[1,1024,3584]{2,1,0:T(8,128)(2,1)}) %all-gather.39.cloned.1.call-update) | async-done | bytes 7340048 | tf_op jit(solution)/vmap(jvp())/squeeze | solution.py:27
  789.4 24.5 fusion.24
  813.9 23.1 fusion.59
  837.0 30.3 fusion.6
  867.2 21.1 fusion.53
  888.4 4.8 fusion.77
  893.2 23.8 convolution_convert_fusion
  917.0 30.2 fusion.9
  947.2 24.8 fusion.20
  972.0 19.8 fusion.49
  992.5 27.1 fusion.40
  1019.7 23.0 convolution_bitcast_fusion.1
  1043.3 23.1 convolution_bitcast_fusion.2
  1066.5 21.4 convolution_bitcast_fusion
  1087.9 30.3 fusion.34
  1118.2 535.0 %fusion.107 = (f32[32,1024]{1,0:T(8,128)S(1)}, f32[32,1024]{1,0:T(8,128)S(1)}) fusion(f32[1,3584,1024]{2,1,0:T(8,128)} %convolution_bitcast_fusion, f32[1,3584,1024]{2,1,0:T(8,128)} %fusion.34), kind=kCustom, calls=%all-reduce-scatter.2 | all-reduce-scatter fusion | flops 8388609 | bytes 29623296
  1655.8 1.9 collective-permute-start.1
  1663.0 1.4 collective-permute-done.1
  1666.1 6.2 collective-permute-start.7
  1672.3 2.7 collective-permute-start.8
  1675.0 1.6 collective-permute-start.9
  1678.0 4.3 collective-permute-start.11
  1682.3 20.2 collective-permute-start.12
  1702.5 13.1 collective-permute-start.13
  1715.6 2.8 collective-permute-start.14
  1718.5 1.9 collective-permute-start
  1720.4 4.6 collective-permute-start.17
  1725.0 5.1 collective-permute-start.18
  1730.1 3.2 collective-permute-start.19
  1733.4 5.1 collective-permute-start.20
  1738.5 2.1 collective-permute-start.21
  1740.6 3.5 collective-permute-start.22
  1745.5 2.7 collective-permute-start.24
  1748.3 2.8 collective-permute-start.25
  1751.1 1.9 collective-permute-start.26
  1754.3 6.7 collective-permute-start.27
  1761.0 3.1 collective-permute-start.28
  1764.1 1.3 collective-permute-start.29
  1766.8 2.7 collective-permute-start.16
  1769.5 7.6 fusion.76
  1777.2 6.4 copy.12
  1783.6 2.7 concatenate
  1786.3 2.7 concatenate.1
  1790.8 477.2 %reduce-scatter.27.cloned.1.call-done = f32[1,8,3584]{2,1,0:T(8,128)} async-done(((f32[1,1024,3584]{2,1,0:T(8,128)}), f32[1,8,3584]{2,1,0:T(8,128)}) %reduce-scatter.27.cloned.1.call-update) | async-done | bytes 114704
  2269.5 721.9 %reduce-scatter.23.cloned.1.call-done = f32[1,8,3584]{2,1,0:T(8,128)} async-done(((f32[1,1024,3584]{2,1,0:T(8,128)}), f32[1,8,3584]{2,1,0:T(8,128)}) %reduce-scatter.23.cloned.1.call-update) | async-done | bytes 114704
  2992.3 723.5 %reduce-scatter.21.cloned.1.call-done = f32[1,8,3584]{2,1,0:T(8,128)} async-done(((f32[1,1024,3584]{2,1,0:T(8,128)}), f32[1,8,3584]{2,1,0:T(8,128)}) %reduce-scatter.21.cloned.1.call-update) | async-done | bytes 114704
  (109 shorter events, 24.5 us)
Async XLA Ops:
  7.2 127.2 %all-gather.29.cloned.1.call-start = ((), (), s32[]{:S(2)}) async-start(), calls=%async_computation.4 | async-start | bytes 7397376 | tf_op jit(solution)/vmap(jvp())/squeeze | solution.py:27
  8.8 247.8 %all-gather.31.cloned.1.call-start = ((), (), s32[]{:S(2)}) async-start(), calls=%async_computation.5 | async-start | bytes 7397376 | tf_op jit(solution)/vmap(jvp())/squeeze | solution.py:27
  10.3 390.0 %all-gather.33.cloned.1.call-start = ((), (), s32[]{:S(2)}) async-start(), calls=%async_computation.6 | async-start | bytes 14794752 | tf_op jit(solution)/vmap(jvp())/squeeze | solution.py:27
  12.3 532.0 %all-gather.37.cloned.1.call-start = ((), (), s32[]{:S(2)}) async-start(), calls=%async_computation.8 | async-start | bytes 14794752 | tf_op jit(solution)/vmap(jvp())/squeeze | solution.py:27
  12.9 653.9 %all-gather.35.cloned.1.call-start = ((), (), s32[]{:S(2)}) async-start(), calls=%async_computation.7 | async-start | bytes 7397376 | tf_op jit(solution)/vmap(jvp())/squeeze | solution.py:27
  13.4 776.0 %all-gather.39.cloned.1.call-start = ((), (), s32[]{:S(2)}) async-start(), calls=%async_computation.9 | async-start | bytes 7397376 | tf_op jit(solution)/vmap(jvp())/squeeze | solution.py:27
  14.0 1775.8 %reduce-scatter.25.cloned.1.call-start = ((), (), s32[]{:S(2)}) async-start(), calls=%async_computation.12 | async-start | bytes 14794752
  424.8 0.6 copy-start.4
  425.4 463.0 %copy-start.6 = (f32[1,1,2048]{2,1,0:T(1,128)}, f32[1,1,2048]{2,1,0:T(1,128)S(1)}, u32[]{:S(2)}) copy-start(f32[1,1,2048]{2,1,0:T(1,128)S(1)} %rsqrt.23) | copy-start | bytes 24580
  718.6 1549.3 %reduce-scatter.27.cloned.1.call-start = ((), (), s32[]{:S(2)}) async-start(), calls=%async_computation.13 | async-start | bytes 14794752
  789.4 24.5 copy-start.2
  867.2 21.1 copy-start.5
  867.2 21.2 copy-start.1
  917.0 55.0 %slice-start = ((s8[7340032]{0:T(1024)(128)(4,1)}), s8[4194304]{0:T(1024)(128)(4,1)S(1)}, s32[]{:S(2)}) async-start(s8[7340032]{0:T(1024)(128)(4,1)} %bitcast.293), calls=%async_computation.14 | async-start | bytes 8388608
  947.2 24.8 copy-start
  947.2 24.8 slice-start.1
  972.0 19.8 copy-start.9
  1019.6 1971.8 %reduce-scatter.23.cloned.1.call-start = ((), (), s32[]{:S(2)}) async-start(), calls=%async_computation.11 | async-start | bytes 14794752
  1042.6 0.7 copy-start.7
  1042.7 2673.2 %reduce-scatter.21.cloned.1.call-start = ((), (), s32[]{:S(2)}) async-start(), calls=%async_computation.10 | async-start | bytes 14794752
  1066.5 21.4 copy-start.3
  1118.2 634.9 %copy-start.10 = (u32[256]{0:T(256)S(1)}, u32[256]{0:T(256)}, u32[]{:S(2)}) copy-start(u32[256]{0:T(256)} %constant.180) | copy-start | bytes 3076
  1118.2 651.3 %copy-start.8 = (f32[1,1,2048]{2,1,0:T(1,128)S(1)}, f32[1,1,2048]{2,1,0:T(1,128)}, u32[]{:S(2)}) copy-start(f32[1,1,2048]{2,1,0:T(1,128)} %get-tuple-element.53) | copy-start | bytes 24580
  1653.2 7.2 collective-permute-start.15
  1654.5 7.2 collective-permute-start.31
  1655.8 8.5 collective-permute-start.1
  1657.8 8.3 collective-permute-start.2
  1659.1 13.2 collective-permute-start.3
  1660.4 14.6 collective-permute-start.4
  1661.7 15.0 collective-permute-start.5
  1664.4 13.6 collective-permute-start.6
  1666.1 16.2 collective-permute-start.7
  1672.3 30.2 collective-permute-start.8
  1675.0 40.6 %collective-permute-start.9 = (bf16[32,1024]{1,0:T(8,128)(2,1)S(1)}, bf16[32,1024]{1,0:T(8,128)(2,1)S(1)}, u32[]{:S(2)}, u32[]{:S(2)}) collective-permute-start(bf16[32,1024]{1,0:T(8,128)(2,1)S(1)} %convert.109), channel_id=1, source_target_pairs={{0,10},{1,11},{2,12},{3,13},{4,14},{5,15},{6,16},{7,17},{8,18},{9,... | collective-permute-start | bytes 196616
  1676.7 41.8 %collective-permute-start.10 = (bf16[32,1024]{1,0:T(8,128)(2,1)S(1)}, bf16[32,1024]{1,0:T(8,128)(2,1)S(1)}, u32[]{:S(2)}, u32[]{:S(2)}) collective-permute-start(bf16[32,1024]{1,0:T(8,128)(2,1)S(1)} %convert.109), channel_id=1, source_target_pairs={{0,11},{1,12},{2,13},{3,14},{4,15},{5,16},{6,17},{7,18},{8,19},{9,... | collective-permute-start | bytes 196616
  1678.0 42.4 %collective-permute-start.11 = (bf16[32,1024]{1,0:T(8,128)(2,1)S(1)}, bf16[32,1024]{1,0:T(8,128)(2,1)S(1)}, u32[]{:S(2)}, u32[]{:S(2)}) collective-permute-start(bf16[32,1024]{1,0:T(8,128)(2,1)S(1)} %convert.109), channel_id=1, source_target_pairs={{0,12},{1,13},{2,14},{3,15},{4,16},{5,17},{6,18},{7,19},{8,20},{9,... | collective-permute-start | bytes 196616
  1682.3 42.7 %collective-permute-start.12 = (bf16[32,1024]{1,0:T(8,128)(2,1)S(1)}, bf16[32,1024]{1,0:T(8,128)(2,1)S(1)}, u32[]{:S(2)}, u32[]{:S(2)}) collective-permute-start(bf16[32,1024]{1,0:T(8,128)(2,1)S(1)} %convert.109), channel_id=1, source_target_pairs={{0,13},{1,14},{2,15},{3,16},{4,17},{5,18},{6,19},{7,20},{8,21},{9,... | collective-permute-start | bytes 196616
  1702.5 27.6 collective-permute-start.13
  1715.6 17.7 collective-permute-start.14
  1718.5 20.0 collective-permute-start
  1720.4 20.2 collective-permute-start.17
  1725.0 19.2 collective-permute-start.18
  1730.1 15.4 collective-permute-start.19
  1733.4 14.9 collective-permute-start.20
  1738.5 12.6 collective-permute-start.21
  1740.6 13.7 collective-permute-start.22
  1744.2 16.8 collective-permute-start.23
  1745.5 18.6 collective-permute-start.24
  1748.3 17.2 collective-permute-start.25
  1751.1 15.7 collective-permute-start.26
  1754.3 31.9 collective-permute-start.27
  1761.0 25.3 collective-permute-start.28
  1764.1 22.1 collective-permute-start.29
  1765.5 20.8 collective-permute-start.30
  1766.8 19.5 collective-permute-start.16
Sparse Core Ops, SparseCore 0:
  11.4 122.8 all-gather.28
  137.8 118.7 all-gather.30
  260.7 139.6 all-gather.32
  404.3 139.9 all-gather.36
  547.6 119.0 all-gather.34
  670.6 118.7 all-gather.38
  792.0 742.2 reduce-scatter.24
  1536.8 731.0 reduce-scatter.26
  2270.5 720.8 reduce-scatter.22
  2993.8 721.9 reduce-scatter.20
where the time goes:
time: 3740 us; the launch traced here: 3720 us
  waiting for transfers between devices  2510 us (67%)
  blocking collectives  535 us (14%)
  matrix products  408 us (11%)
  starting transfers between devices  113 us (3%)
  other arithmetic  108 us (3%)
    unnamed x46, waiting for transfers between devices  1930 us
    squeeze x6, waiting for transfers between devices, stack(): h = layer(h, {name: w[number] for name, w in weights.items()})  586 us
    unnamed x1, blocking collectives  535 us
    dot_general x6, matrix products, layer(): up = jnp.dot(a, w['w_up'], preferred_element_type=jnp.float32)  150 us
    dot_general x6, matrix products, layer(): gate = jnp.dot(a, w['w_gate'], preferred_element_type=jnp.float32)  135 us
    dot_general x5, matrix products, matmul(): jnp.dot(a, w, preferred_element_type=jnp.float32).astype(jnp.bfloat16)  123 us
    unnamed x36, starting transfers between devices  113 us
    unnamed x6, other arithmetic  86.3 us
  transfers between devices with their start and end apart: 42, of which 11 were waited for; matrix products, arithmetic and copies ran while one was open for 29% of the time, Pallas kernels for 0%

commit v1 on v0

v1 whole, which is shorter than its diff:
```python
import jax
import jax.numpy as jnp
from jax import lax
from jax.experimental import pallas as pl
from jax.experimental.pallas import tpu as pltpu
from jax.sharding import PartitionSpec as P

T, D, FF, L = 2048, 1024, 3584, 2
X, Y, Z = 4, 4, 8
C, NC = 512, 7
H, LANES = C // 2, 128
TM = 1024
HT = TM // 2
BOTH = range(2)
NR = T // TM
PER = NR + 2
bf16, f32 = jnp.bfloat16, jnp.float32
UNITS = L * NC
SIZE = {"x": X, "y": Y, "z": Z}
RS_AXES = (("x", "y", "z"), ("y", "x", "z"), ("z", "x", "y"))
AG_AXES = tuple(tuple(reversed(a)) for a in RS_AXES)
HALVES = (((128, C), (2, 64, C), (64, C)), ((32, C), (32, C), (16, C)))
GU_PLACE = (4, 6, 9, 10, 13, 16)
PLACE = (GU_PLACE, GU_PLACE, (3, 4, 6, 8, 10, 12, 14, 16))
GU_TICK = (0, 2, 3, 5, 7, 8)
TICK = (GU_TICK, GU_TICK, (0, 1, 3, 4, 5, 6, 7, 8))
G1 = 9
G2 = G1 + NR * NC + NR
G3 = G2 + PER * NC
G4 = G3 + PER * NC
GEND = G4 + 13
LATE = 2
AG_SLOTS, SEMS = 5, 19
MESH = pl.DeviceIdType.MESH


def rs_stages(m):
    return [(p, k) for p in (0, 1) for k in range(1, SIZE[RS_AXES[m][p]] // 2 + 1)] + [(2, 1)]


def ag_stages(m):
    return [(0, 1), (1, 1)] + [(2, k) for k in range(1, SIZE[AG_AXES[m][2]] // 2 + 1)] + [(3, 1)]


def dot(a, b, ca=1, cb=0):
    return lax.dot_general(a, b, (((ca,), (cb,)), ((), ())), preferred_element_type=f32)


def rows(start, size):
    return pl.ds(start if isinstance(start, int) else pl.multiple_of(start, size), size)


def parts(n, size):
    return lax.div(n, size), lax.rem(n, size)


def norm_rows(h):
    wide = h.astype(f32)
    scale = lax.rsqrt(jnp.mean(wide * wide, -1, keepdims=True) + 1e-6)
    return (wide * scale).astype(bf16)


def norm_back(h, da):
    wide, da = h.astype(f32), da.astype(f32)
    scale = lax.rsqrt(jnp.mean(wide * wide, -1, keepdims=True) + 1e-6)
    along = jnp.sum(da * wide, -1, keepdims=True)
    return (da * scale - wide * (along * (scale * scale * scale) * (1.0 / D))).astype(bf16)


def kernel(x_hbm, dy_hbm, gate_hbm, up_hbm, down_hbm,
           dx_hbm, og_hbm, ou_hbm, od_hbm, wg_hbm, wu_hbm, wd_hbm, a0_hbm, gu_hbm, late_hbm,
           a, dy, h, acc, wg, wu, wd, act, dg, du, gst, ust, ug, uu, ud,
           halves, fulls, zb, r3, res, raw, sw, quarter, outd, half, dbuf,
           isem, wsem, gsem, lsem, ags, agr, rss, rsr, psem):
    rep, dp = lax.axis_index("rep"), lax.axis_index("dp")
    mx, left = parts(dp, Y * Z)
    my, mz = parts(left, Z)
    zp, zh = parts(mz, 2)
    me = {"x": mx, "y": my, "z": mz}
    stride = {"x": Y * Z, "y": Z, "z": 1}
    ring = {axis: [lax.rem(me[axis] + o, n) for o in range(n)] for axis, n in SIZE.items()}
    peer = {axis: [{"dp": dp + (v - me[axis]) * stride[axis]} for v in vs] for axis, vs in ring.items()}
    partner = {"rep": 1 - rep}
    twin = {"dp": dp + 1 - 2 * zh}

    def coord(axis, offset):
        return ring[axis][offset % SIZE[axis]]

    def near(axis, offset):
        return peer[axis][offset % SIZE[axis]]

    def remote(src, dst, ssem, rsem, device):
        return pltpu.make_async_remote_copy(src, dst, ssem, rsem, device_id=device, device_id_type=MESH)

    barrier = pltpu.get_barrier_semaphore()
    everyone = [partner] + [d for axis in SIZE for d in peer[axis][1:]]
    for device in everyone:
        pl.semaphore_signal(barrier, inc=1, device_id=device, device_id_type=MESH)

    def my_columns(side):
        return rows(C * side + H * rep, H)

    cx = pltpu.make_async_copy(x_hbm, h, isem.at[0])
    cdy = pltpu.make_async_copy(dy_hbm, dy, isem.at[1])
    ca0 = pltpu.make_async_copy(a, a0_hbm, isem.at[5])
    ca = pltpu.make_async_copy(a0_hbm, a, isem.at[2])
    cdx = pltpu.make_async_copy(dy, dx_hbm, isem.at[1])
    loads = [pltpu.make_async_copy(gate_hbm, raw.at[0], isem.at[2]), pltpu.make_async_copy(up_hbm, raw.at[1], isem.at[3]),
             pltpu.make_async_copy(down_hbm.at[:, :, my_columns(zh)], quarter.at[0], isem.at[4])]
    own = [
        pltpu.make_async_copy(sw.at[0], wg_hbm.at[:, rep, mx, rows(64 * my + 8 * mz, 8)], isem.at[2]),
        pltpu.make_async_copy(sw.at[1], wu_hbm.at[:, rep, mx, rows(64 * my + 8 * mz, 8)], isem.at[3]),
        pltpu.make_async_copy(sw.at[2], wd_hbm.at[:, zh, rep, rows(128 * zp + 32 * mx + 8 * my, 8)], isem.at[4]),
    ]
    swap = remote(down_hbm.at[:, :, my_columns(1 - zh)], quarter.at[1], psem.at[0, 0], psem.at[1, 0], twin)

    group = lax.shift_right_logical(lax.broadcasted_iota(jnp.int32, (8, 128), 1), 3)

    def arrange(n, _):
        l, q = parts(n, NC * 2)
        j, e = parts(q, 2)
        w = 8 * (7 * (2 * rep + e) + j)
        for m in BOTH:
            out = jnp.zeros((8, LANES), f32)
            for xy in range(X * Y):
                at = 224 * xy + w
                lanes = pltpu.roll(raw[m, l, :, rows(lax.shift_right_logical(at, 7) * LANES, LANES)].astype(f32),
                                   (8 * xy - at) & 127, 1)
                out = jnp.where(group == xy, lanes, out)
            sw[m, l * NC + j, :, rows(LANES * e, LANES)] = out.astype(bf16)
        return 0

    def begin():
        for c in loads:
            c.start()
        cx.start()
        cdy.start()
        for c in loads:
            c.wait()
        lax.fori_loop(0, UNITS, arrange, 0)
        pl.semaphore_wait(barrier, len(everyone))
        swap.start()
        lax.fori_loop(UNITS, UNITS * 2, arrange, 0)
        for c in own[:2]:
            c.start()
        swap.wait()
        for l in range(L):
            for side in BOTH:
                @pl.when(zh == side)
                def _():
                    for b in BOTH:
                        dbuf[pl.ds(28 * (side ^ b), 28), :H] = quarter[b, l].astype(f32)
            for j in range(NC):
                sw[2, l * NC + j] = dbuf[8 * j:8 * j + 8, :H].astype(bf16)
        own[2].start()

    begin()

    def ag_block(m, u, p, v, side):
        def some(start, n):
            return rows(start, n) if side is None else rows(start + n // 2 * side, n // 2)
        if m == 2:
            if p == 0:
                return wd_hbm.at[u, zh, rep, rows(128 * zp + 32 * mx + 8 * v, 8)]
            if p == 1:
                return wd_hbm.at[u, zh, rep, rows(128 * zp + 32 * v, 32)]
            pair, odd = parts(v, 2)
            return wd_hbm.at[u, odd, rep, some(128 * pair, 128)]
        w = (wg_hbm, wu_hbm)[m]
        if p == 0:
            return w.at[u, rep, mx, rows(64 * my + 8 * v, 8)]
        if m == 0:
            return w.at[u, rep, mx, rows(64 * v, 64)] if p == 1 else w.at[u, rep, v, some(0, 256)]
        if p == 1:
            return w.at[u, rep, v, rows(64 * my, 64)]
        return w.at[u, rep, some(0, X), rows(64 * v, 64)]

    def ag_copies(m, u, s):
        slot = lax.rem(u, AG_SLOTS)
        p, k = ag_stages(m)[s]

        def sems(n):
            return ags.at[slot, m, n], agr.at[slot, m, n]
        if p == 3:
            ref = (wg_hbm.at[u, rep], wu_hbm.at[u, rep], wd_hbm.at[u, :, rep])[m]
            return [remote(ref, ref, *sems(SEMS - 1), partner)]
        axis = AG_AXES[m][p]
        if p < 2:
            ref = ag_block(m, u, p, me[axis], None)
            return [remote(sw.at[m, u] if p == 0 else ref, ref, *sems(7 * p + o - 1), near(axis, o))
                    for o in range(1, SIZE[axis])]
        out = []
        for d, sign in enumerate((1, -1)):
            ref = ag_block(m, u, p, coord(axis, -sign * (k - 1)), d if k == SIZE[axis] // 2 else None)
            out.append(remote(ref, ref, *sems(8 + 2 * k + d), near(axis, sign)))
        return out

    def ag_stage(u, here):
        for m, s in here:
            if s > 0:
                for c in ag_copies(m, u, s - 1):
                    c.wait()
        for m, s in here:
            if s < len(ag_stages(m)):
                for c in ag_copies(m, u, s):
                    c.start()

    def ag_tick(t):
        for parity in BOTH:
            @pl.when(lax.rem(t, 2) == parity)
            def _():
                for at in range(parity, G1, 2):
                    here = [(m, s) for m in range(3) for s, place in enumerate(TICK[m]) if place == at]

                    @pl.when((t >= at) & (t < at + 2 * UNITS))
                    def _():
                        ag_stage(lax.div(t - at, 2), here)

    def rs_region(m, i, p, v, side):
        slot = lax.rem(i, 3)

        def some(start, n):
            return rows(start, n) if side is None else rows(start + n // 2 * side, n // 2)
        if p == 2:
            return zb[m].at[lax.rem(i, 2), v]
        if m == 0:
            return ug.at[slot, some(256 * v, 256) if p == 0 else some(256 * mx + 64 * v, 64)]
        if m == 1:
            return uu.at[slot, some(0, X), rows(64 * v, 64)] if p == 0 else uu.at[slot, v, some(64 * my, 64)]
        if p == 0:
            pair, odd = parts(v, 2)
            return ud.at[slot, some(128 * pair, 128), rows(C * odd, C)]
        return ud.at[slot, some(128 * zp + 32 * v, 32), rows(C * zh, C)]

    def rs_landing(m, i, p, k, d):
        slot = lax.rem(i, 2)
        if p == 2:
            return r3[m].at[slot, d]
        return halves[p][m].at[slot, d] if k == 1 else fulls[p][m].at[slot, k - 2, d]

    def rs_copies(m, i, s):
        p, k = rs_stages(m)[s]
        axis = RS_AXES[m][p]
        slot = lax.rem(i, 2)

        def copy(v, side, d, n, device):
            return remote(rs_region(m, i, p, v, side), rs_landing(m, i, p, k, d), rss.at[slot, m, n], rsr.at[slot, m, n], device)
        if p == 2:
            return [copy(coord(axis, o), None, o - 1, 11 + o, near(axis, o)) for o in range(1, SIZE[axis])]
        return [copy(coord(axis, sign * (SIZE[axis] // 2 + 1 - k)), d if k == 1 else None, d, 2 * s + d, near(axis, sign))
                for d, sign in enumerate((1, -1))]

    def add_tiles(dst, srcs, put):
        *lead, n, _ = dst.shape
        t = min(n, 64)
        count = (lead[0] if lead else 1) * (n // t)

        def tile(q):
            b, r = parts(q, n // t)
            ix = (b, rows(r * t, t)) if lead else (rows(q * t, t),)
            put(ix, sum((ref[ix].astype(f32) for ref in srcs), dst[ix].astype(f32)))
        if count == 1:
            tile(0)
        else:
            lax.fori_loop(0, count, lambda q, _: (tile(q), 0)[1], 0)

    def rs_stage(m, i, s):
        todo = rs_stages(m)
        if s > 0:
            for c in rs_copies(m, i, s - 1):
                c.wait()
            p, k = todo[s - 1]
            axis = RS_AXES[m][p]
            n = SIZE[axis]
            if p == 2:
                total = zb[m][lax.rem(i, 2), me[axis]].astype(f32)
                for o in range(n - 1):
                    total += r3[m][lax.rem(i, 2), o].astype(f32)
                res[m, i] = total.astype(bf16)
            elif k < n // 2:
                for d, sign in enumerate((1, -1)):
                    reg = rs_region(m, i, p, coord(axis, sign * (n // 2 - k)), d if k == 1 else None)

                    def put(ix, v, reg=reg):
                        reg[ix] = v.astype(bf16)
                    add_tiles(reg, [rs_landing(m, i, p, k, d)], put)
            else:
                mine = rs_region(m, i, p, me[axis], None)

                def put(ix, v):
                    if p == 0:
                        mine[ix] = v.astype(bf16)
                    else:
                        last = SIZE[RS_AXES[m][2]]
                        zb[m][lax.rem(i, 2)] = v.reshape(last, 8, C).astype(bf16)
                add_tiles(mine, [rs_landing(m, i, p, k, d) for d in BOTH], put)
        if s < len(todo):
            for c in rs_copies(m, i, s):
                c.start()

    def rs_hook(i, sub):
        for at in range(PER):
            @pl.when(sub == at)
            def _():
                for back in range(4, -1, -1):
                    here = [(m, s) for m in range(3) for s, place in enumerate(PLACE[m]) if place == at + PER * back]
                    if here:
                        @pl.when((i >= back) & (i < back + UNITS))
                        def _():
                            for m, s in here:
                                rs_stage(m, i - back, s)

    def send_half(l):
        return remote(half.at[0, l], half.at[1, l], psem.at[0, 1 + l], psem.at[1, 1 + l], twin)

    def collect(l):
        i0 = (L - 1 - l) * NC

        def tile(m, _):
            for t in range(FF // LANES):
                out = jnp.zeros((8, LANES), f32)
                for q in range(X * Y):
                    xy, w = divmod(16 * t + q, 28)
                    quad, j = divmod(w, NC)
                    lanes = pltpu.roll(res[m, i0 + j, :, LANES * quad:LANES * (quad + 1)].astype(f32), (8 * q - 8 * xy) % LANES, 1)
                    out = jnp.where(group == q, lanes, out)
                raw[m, l, :, LANES * t:LANES * (t + 1)] = out.astype(bf16)
            return 0
        for j in range(NC):
            dbuf[8 * j:8 * j + 8, :] = res[2, i0 + j].astype(f32)
        for side in BOTH:
            @pl.when(zh == side)
            def _():
                half[0, l] = dbuf[28 - 28 * side:56 - 28 * side, :].astype(bf16)
                outd[l, :, C * side:C * side + C] = dbuf[28 * side:28 * side + 28, :].astype(bf16)
        send_half(l).start()
        lax.fori_loop(0, 2, tile, 0)

    def w_copies(u, slot, down):
        if down:
            return [pltpu.make_async_copy(wd_hbm.at[u, q, c], wd.at[slot, :, pl.ds(C * q + H * c, H)], wsem.at[slot, 2])
                    for q in BOTH for c in BOTH]
        return [pltpu.make_async_copy(far.at[u, c], ref.at[slot, :, :, pl.ds(H * c, H)], wsem.at[slot, b])
                for b, (far, ref) in enumerate(((wg_hbm, wg), (wu_hbm, wu))) for c in BOTH]

    def w_start(u, slot, down):
        for c in w_copies(u, slot, down):
            c.start()

    def w_wait(slot, down):
        for b, ref in ((2, wd),) if down else ((0, wg), (1, wu)):
            pltpu.make_async_copy(ref.at[slot], ref.at[slot], wsem.at[slot, b]).wait()

    def gate_up(slot):
        return wg[slot].reshape(D, C), wu[slot].reshape(D, C)

    def gu_copies(n, back):
        slot = lax.rem(n, 2)
        j, r = parts(n, NR)
        out = []
        for b, st in enumerate((gst, ust)):
            far = gu_hbm.at[j, b, rows(r * TM, TM)]
            out.append(pltpu.make_async_copy(*((far, st.at[slot]) if back else (st.at[slot], far)), gsem.at[slot, b]))
        return out

    def add_da(rs, dgb, dub, slot):
        wgs, wus = gate_up(slot)
        acc[rs, :] += dot(dgb, wgs, 1, 1) + dot(dub, wus, 1, 1)

    def back_rows(gates, ups, halves_, slot, da):
        dacts = [dot(dy[rs, :], wd[slot], 1, 1).astype(bf16) for rs in halves_]
        for gate, up, dact, rs in zip(gates, ups, dacts, halves_):
            g, u, dact = gate[...], up[...], dact.astype(f32)
            sig = 1.0 / (1.0 + jnp.exp(-g))
            sl = g * sig
            act[rs, :] = (sl * u).astype(bf16)
            dub = (dact * sl).astype(bf16)
            dgb = (dact * u * (sig + sl * (1.0 - sig))).astype(bf16)
            du[rs, :] = dub
            dg[rs, :] = dgb
            if da:
                add_da(rs, dgb, dub, slot)

    def kept_rows(st):
        return [[ref.at[st, q * HT:q * HT + HT] for q in BOTH] for ref in (gst, ust)]

    def late_copies(back):
        pairs = [(v, late_hbm.at[b]) for b, v in enumerate((dg, du))]
        return [pltpu.make_async_copy(*(p[::-1] if back else p), lsem.at[b]) for b, p in enumerate(pairs)]

    def tiles(f):
        lax.fori_loop(0, T // 256, lambda q, _: (f(rows(q * 256, 256)), 0)[1], 0)

    def clear(rs):
        acc[rs, :] = jnp.zeros((256, D), f32)

    def enter(rs, new):
        h[rs, :] = new
        a[rs, :] = norm_rows(new)
        clear(rs)

    def leave(rs):
        dy[rs, :] = dy[rs, :] + norm_back(h[rs, :], acc[rs, :].astype(bf16))
        clear(rs)

    def step(g, _):
        backward = g >= G2
        i, sub = parts(jnp.maximum(g - G2, 0), PER)
        j1, r1 = parts(g + 1, NR)
        cc = jnp.where(backward, NC + i, j1 - (G1 + 1) // NR)
        r = jnp.where(backward, sub, r1)
        slot = lax.rem(cc + 2 * NC, 2)
        n1 = g - G1
        rs = rows(lax.rem(r, NR) * TM, TM)
        quarters = [rows(lax.rem(r, NR) * TM + q * HT, HT) for q in BOTH]

        @pl.when((g < G2 - NR) | (backward & (g < 2 * UNITS + G1)))
        def _():
            @pl.when(g == 1)
            def _():
                for c in own:
                    c.wait()
            with jax.named_scope("gather"):
                ag_tick(jnp.where(backward, g - NR, g))

        @pl.when(r == 0)
        def _():
            @pl.when(g == 1)
            def _():
                cx.wait()
                tiles(lambda rs: enter(rs, h[rs, :]))
                ca0.start()

            @pl.when(g == G1 + NR)
            def _():
                tiles(clear)

            @pl.when(g == G2)
            def _():
                for n in range(NC * NR - 2, NC * NR):
                    for c in gu_copies(n, False):
                        c.wait()
                ca0.wait()
                cdy.wait()
                with jax.named_scope("enter"):
                    tiles(lambda rs: enter(rs, h[rs, :] + acc[rs, :].astype(bf16)))

            @pl.when(g == G3)
            def _():
                ca.start()
                for c in gu_copies(0, True):
                    c.start()
                with jax.named_scope("leave"):
                    tiles(leave)
                cx.start()

            @pl.when((g < G4) & (cc >= 0))
            def _():
                with jax.named_scope("weights"):
                    @pl.when((cc < NC) | backward)
                    def _():
                        w_wait(slot, False)

                    @pl.when(backward)
                    def _():
                        w_wait(slot, True)

                    @pl.when((cc > 0) & (g < G2))
                    def _():
                        w_wait(1 - slot, True)

        @pl.when((r == 1) & (cc >= -1) & (cc < 3 * NC))
        def _():
            nxt = cc + 1

            @pl.when((cc < 3 * NC - 1) & ((cc < NC) | backward))
            def _():
                w_start(jnp.where(nxt < UNITS, nxt, nxt - UNITS), 1 - slot, False)

            @pl.when((cc < 3 * NC - 1) & backward)
            def _():
                w_start(jnp.where(nxt < UNITS, nxt, nxt - UNITS), 1 - slot, True)

            @pl.when((cc >= 0) & (g < G2))
            def _():
                w_start(cc, slot, True)

        @pl.when((n1 >= 0) & (g < G2))
        def _():
            st = lax.rem(n1, 2)

            @pl.when((n1 >= 2) & (n1 < NC * NR))
            def _():
                for c in gu_copies(n1 - 2, False):
                    c.wait()

            @pl.when(cc < NC)
            def _():
                with jax.named_scope("row1"):
                    ar = a[rs, :]
                    wgs, wus = gate_up(slot)
                    gst[st] = dot(ar, wgs)
                    ust[st] = dot(ar, wus)
                    acc[rs, :] += dot(act[rs, :], wd[1 - slot])
                    gate = gst[st]
                    sig = 1.0 / (1.0 + jnp.exp(-gate))
                    act[rs, :] = (gate * sig * ust[st]).astype(bf16)
                for c in gu_copies(n1, False):
                    c.start()

            @pl.when(cc == NC)
            def _():
                acc[rs, :] += dot(act[rs, :], wd[1 - slot])

        @pl.when(backward)
        def _():
            with jax.named_scope("scatter"):
                rs_hook(i, sub)
            mine = lax.rem(i, 3)

            @pl.when((sub < NR) & (g < G3))
            def _():
                with jax.named_scope("row2"):
                    wgs, wus = gate_up(slot)
                    gst[0] = dot(a[rs, :], wgs)
                    ust[0] = dot(a[rs, :], wus)
                    back_rows(*kept_rows(0), quarters, slot, True)

            @pl.when((sub < NR) & (g >= G3) & (g < G4))
            def _():
                n = (i - NC) * NR + sub
                for c in gu_copies(n, True):
                    c.wait()

                @pl.when(n + 1 < NC * NR)
                def _():
                    for c in gu_copies(n + 1, True):
                        c.start()
                kept = kept_rows(lax.rem(n, 2))

                @pl.when(i < UNITS - LATE)
                def _():
                    with jax.named_scope("row3"):
                        back_rows(*kept, quarters, slot, True)

                @pl.when((i >= UNITS - LATE) & (n == NR * (NC - 1)))
                def _():
                    for c in late_copies(False):
                        c.wait()

                @pl.when(i >= UNITS - LATE)
                def _():
                    with jax.named_scope("row3late"):
                        back_rows(*kept, quarters, slot, False)

            @pl.when((sub == NR) & (g < G4))
            def _():
                @pl.when(g == G3 + NR)
                def _():
                    ca.wait()

                @pl.when(i == UNITS - LATE)
                def _():
                    for c in late_copies(False):
                        c.start()
                with jax.named_scope("dd"):
                    ud[mine] = dot(act[...], dy[...], 0, 0).astype(bf16)

            @pl.when((sub == NR + 1) & (g < G4))
            def _():
                with jax.named_scope("dw"):
                    ug[mine] = dot(a[...], dg[...], 0, 0).astype(bf16)
                    uu[mine] = dot(a[...], du[...], 0, 0).astype(bf16).reshape(X, H, C)

            @pl.when(g >= G4)
            def _():
                n = g - G4

                @pl.when(n == NR + 1)
                def _():
                    for c in late_copies(True):
                        c.wait()

                @pl.when((n < NR) | ((n > NR) & (n <= 2 * NR)))
                def _():
                    late, q = parts(n, NR + 1)
                    rs = rows(q * TM, TM)
                    with jax.named_scope("late"):
                        add_da(rs, dg[rs, :], du[rs, :], late)

                @pl.when(n == NR - 1)
                def _():
                    for c in late_copies(True):
                        c.start()

                @pl.when(n == NR)
                def _():
                    cx.wait()

                @pl.when((n == NR) | (g == GEND - 1))
                def _():
                    with jax.named_scope("collect"):
                        collect(jnp.where(n == NR, 1, 0))

                @pl.when(n == 2 * NR + 1)
                def _():
                    tiles(leave)
                    cdx.start()
        return 0

    lax.fori_loop(0, GEND, step, 0)
    ends = [pltpu.make_async_copy(raw.at[0], og_hbm, isem.at[2]), pltpu.make_async_copy(raw.at[1], ou_hbm, isem.at[3]),
            pltpu.make_async_copy(outd, od_hbm, isem.at[4])]
    for c in ends[:2]:
        c.start()
    for l in range(L):
        send_half(l).wait()
        outd[l, :, rows(C * (1 - zh), C)] = half[1, l]
    ends[2].start()
    for c in ends:
        c.wait()
    cdx.wait()


def mega(x, dy, gate, up, down):
    S = jax.ShapeDtypeStruct
    V = pltpu.VMEM
    DMA = pltpu.SemaphoreType.DMA
    hbm = pl.BlockSpec(memory_space=pl.ANY)
    outs = [S((T, D), bf16), S((L, 8, FF), bf16), S((L, 8, FF), bf16), S((L, 28, D), bf16),
            *[S((UNITS, 2, X, H, H), bf16)] * 2, S((UNITS, 2, 2, C, H), bf16),
            S((T, D), bf16), S((NC, 2, T, C), f32), S((2, T, C), bf16)]
    scratch = [
        *[V((T, D), bf16)] * 3, V((T, D), f32),
        *[V((2, X, H, C), bf16)] * 2, V((2, C, D), bf16),
        *[V((T, C), bf16)] * 3, *[V((2, TM, C), f32)] * 2,
        V((3, D, C), bf16), V((3, X, H, C), bf16), V((3, C, D), bf16),
        tuple(tuple(V((2, 2, *s), bf16) for s in shapes) for shapes in HALVES),
        tuple(tuple(V((2, SIZE[RS_AXES[m][p]] // 2 - 1, 2, 2 * s[0], *s[1:]), bf16) for m, s in enumerate(shapes))
              for p, shapes in enumerate(HALVES)),
        tuple(V((2, SIZE[axes[2]], 8, C), bf16) for axes in RS_AXES),
        tuple(V((2, SIZE[axes[2]] - 1, 8, C), bf16) for axes in RS_AXES),
        V((3, UNITS, 8, C), bf16), V((2, L, 8, FF), bf16), V((3, UNITS, 8, H), bf16), V((2, L, 28, H), bf16),
        V((L, 28, D), bf16), V((2, L, 28, C), bf16), V((56, C), f32),
        DMA((6,)), DMA((2, 3)), DMA((2, 2)), DMA((2,)), *[DMA((AG_SLOTS, 3, SEMS))] * 2, *[DMA((2, 3, SEMS))] * 2,
        DMA((2, 3)),
    ]
    return pl.pallas_call(
        kernel, out_shape=outs, in_specs=[hbm] * 5, out_specs=[hbm] * len(outs), scratch_shapes=scratch, name="mega",
        compiler_params=pltpu.CompilerParams(collective_id=0, has_side_effects=True, vmem_limit_bytes=67043328),
    )(x, dy, gate, up, down)[:4]


def body(x, dy, *weights):
    dx, *by_weights = mega(x[0], dy[0], *weights)
    return (dx[None], *by_weights)


def solution(mesh):
    rows_, seq, grad = P(None, "dp", None), P(("rep", "dp"), None, None), P("rep", "dp", None)
    return jax.shard_map(body, mesh=mesh, in_specs=(seq, seq, rows_, rows_, rows_),
                         out_specs=(seq, grad, grad, grad), check_vma=False)
```

time: 3740 us -> 437 us (0.12)
  waiting for transfers between devices: 2510 us -> 0 us
  blocking collectives: 535 us -> 0 us
  Pallas kernels: 0 us -> 426 us
  matrix products: 408 us -> 0 us
  starting transfers between devices: 113 us -> 0 us
  other arithmetic: 108 us -> 0 us
    unnamed x46 -> x0, waiting for transfers between devices: 1930 us -> none
    squeeze x6 -> x0, waiting for transfers between devices: 586 us -> none  [stack(): h = layer(h, {name: w[number] for name, w in weights.items()})]
    unnamed x1 -> x0, blocking collectives: 535 us -> none
    pallas_call x0 -> x1, Pallas kernels: none -> 426 us  [mega(): pl.pallas_call(kernel, out_shape=outs, in_specs=[hbm] * 5, out_specs=[hbm...]
    dot_general x17 -> x0, matrix products: 408 us -> none  [the longest x6 150 us: layer(): up = jnp.dot(a, w['w_up'], preferred_element_type=jnp.float32)]
    unnamed x36 -> x0, starting transfers between devices: 113 us -> none
    unnamed x6 -> x0, other arithmetic: 86.3 us -> none
  transfers between devices with their start and end apart: 42 -> 0, of which waited for: 11 -> 0; matrix products, arithmetic and copies ran while one was open for 29% -> 0% of each run, Pallas kernels for 0% -> 0%
where the time goes in v1:
time: 437 us; the launch traced here: 436 us
  Pallas kernels  426 us (97%)
  local copies, waits for them, and re-layouts  9.22 us (2%)
    pallas_call x1, Pallas kernels, mega(): pl.pallas_call(kernel, out_shape=outs, in_specs=[hbm] * 5, out_specs=[hbm...  426 us
    unnamed x9, local copies, waits for them, and re-layouts  9.22 us

profile of v1, /device:TPU:64, one launch (start us, length us, event | category | flops | bytes accessed | tf_op | source)
XLA Modules:
  0.0 436.4 jit_solution(9213027386309886211)
XLA Ops:
  0.6 1.6 copy.9.down_hbm
  2.2 426.5 %mega.1 = (bf16[2048,1024]{1,0:T(8,128)(2,1)}, bf16[2,8,3584]{2,1,0:T(8,128)(2,1)}, bf16[2,8,3584]{2,1,0:T(8,128)(2,1)}, bf16[2,28,1024]{2,1,0:T(8,128)(2,1)}, b...) custom-call(bf16[2048,1024]{1,0:T(8,128)(2,1)} %bitcast.3, ...), custom_call_target="tpu_custom_call" | custom-call | tf_op jit(solution)/shard_map/mega/pallas_call | solution.py:648
  428.7 1.7 copy.10
  430.4 0.0 copy-start.1
  430.4 0.0 copy-start
  430.4 4.7 %copy.14 = bf16[1,2048,1024]{2,1,0:T(8,128)(2,1)} copy(bf16[1,2048,1024]{2,1,0:T(8,128)(2,1)} %bitcast.5) | data formatting | bytes 8388608
  435.1 0.0 copy-done.1
  435.1 0.6 copy.15
  435.7 0.0 copy-done
  435.7 0.6 copy.16
Async XLA Ops:
  430.4 4.7 %copy-start.1 = (bf16[2,8,3584]{2,1,0:T(8,128)(2,1)S(1)}, bf16[2,8,3584]{2,1,0:T(8,128)(2,1)}, u32[]{:S(2)}) copy-start(bf16[2,8,3584]{2,1,0:T(8,128)(2,1)} %get-tuple-element.21) | copy-start | bytes 344068
  430.4 5.3 %copy-start = (bf16[2,8,3584]{2,1,0:T(8,128)(2,1)S(1)}, bf16[2,8,3584]{2,1,0:T(8,128)(2,1)}, u32[]{:S(2)}) copy-start(bf16[2,8,3584]{2,1,0:T(8,128)(2,1)} %get-tuple-element.22) | copy-start | bytes 344068

commit v2 on v1

--- a/solution.py
+++ b/solution.py
@@ -11,7 +11,7 @@
 H, LANES = C // 2, 128
 TM = 1024
 HT = TM // 2
-BOTH = range(2)
+BOTH, MATRICES = range(2), range(3)
 NR = T // TM
 PER = NR + 2
 bf16, f32 = jnp.bfloat16, jnp.float32
@@ -20,8 +20,8 @@
 RS_AXES = (("x", "y", "z"), ("y", "x", "z"), ("z", "x", "y"))
 AG_AXES = tuple(tuple(reversed(a)) for a in RS_AXES)
 HALVES = (((128, C), (2, 64, C), (64, C)), ((32, C), (32, C), (16, C)))
-GU_PLACE = (4, 6, 9, 10, 13, 16)
-PLACE = (GU_PLACE, GU_PLACE, (3, 4, 6, 8, 10, 12, 14, 16))
+GU_PLACE = (4, 6, 9, 11, 13, 16)
+PLACE = (GU_PLACE, GU_PLACE, (3, 4, 7, 9, 11, 12, 14, 16))
 GU_TICK = (0, 2, 3, 5, 7, 8)
 TICK = (GU_TICK, GU_TICK, (0, 1, 3, 4, 5, 6, 7, 8))
 G1 = 9
@@ -29,7 +29,7 @@
 G3 = G2 + PER * NC
 G4 = G3 + PER * NC
 GEND = G4 + 13
-LATE = 2
+LATE = 4
 AG_SLOTS, SEMS = 5, 19
 MESH = pl.DeviceIdType.MESH
 
@@ -42,6 +42,10 @@
     return [(0, 1), (1, 1)] + [(2, k) for k in range(1, SIZE[AG_AXES[m][2]] // 2 + 1)] + [(3, 1)]
 
 
+def odd_of(n):
+    return lax.rem(n, 2)
+
+
 def dot(a, b, ca=1, cb=0):
     return lax.dot_general(a, b, (((ca,), (cb,)), ((), ())), preferred_element_type=f32)
 
@@ -54,15 +58,18 @@
     return lax.div(n, size), lax.rem(n, size)
 
 
+def rms_scale(wide):
+    return lax.rsqrt(jnp.mean(wide * wide, -1, keepdims=True) + 1e-6)
+
+
 def norm_rows(h):
     wide = h.astype(f32)
-    scale = lax.rsqrt(jnp.mean(wide * wide, -1, keepdims=True) + 1e-6)
-    return (wide * scale).astype(bf16)
+    return (wide * rms_scale(wide)).astype(bf16)
 
 
 def norm_back(h, da):
     wide, da = h.astype(f32), da.astype(f32)
-    scale = lax.rsqrt(jnp.mean(wide * wide, -1, keepdims=True) + 1e-6)
+    scale = rms_scale(wide)
     along = jnp.sum(da * wide, -1, keepdims=True)
     return (da * scale - wide * (along * (scale * scale * scale) * (1.0 / D))).astype(bf16)
 
@@ -129,32 +136,6 @@
                 out = jnp.where(group == xy, lanes, out)
             sw[m, l * NC + j, :, rows(LANES * e, LANES)] = out.astype(bf16)
         return 0
-
-    def begin():
-        for c in loads:
-            c.start()
-        cx.start()
-        cdy.start()
-        for c in loads:
-            c.wait()
-        lax.fori_loop(0, UNITS, arrange, 0)
-        pl.semaphore_wait(barrier, len(everyone))
-        swap.start()
-        lax.fori_loop(UNITS, UNITS * 2, arrange, 0)
-        for c in own[:2]:
-            c.start()
-        swap.wait()
-        for l in range(L):
-            for side in BOTH:
-                @pl.when(zh == side)
-                def _():
-                    for b in BOTH:
-                        dbuf[pl.ds(28 * (side ^ b), 28), :H] = quarter[b, l].astype(f32)
-            for j in range(NC):
-                sw[2, l * NC + j] = dbuf[8 * j:8 * j + 8, :H].astype(bf16)
-        own[2].start()
-
-    begin()
 
     def ag_block(m, u, p, v, side):
         def some(start, n):
@@ -207,22 +188,62 @@
 
     def ag_tick(t):
         for parity in BOTH:
-            @pl.when(lax.rem(t, 2) == parity)
+            @pl.when(odd_of(t) == parity)
             def _():
                 for at in range(parity, G1, 2):
-                    here = [(m, s) for m in range(3) for s, place in enumerate(TICK[m]) if place == at]
+                    here = [(m, s) for m in MATRICES for s, place in enumerate(TICK[m]) if place == at]
 
                     @pl.when((t >= at) & (t < at + 2 * UNITS))
                     def _():
                         ag_stage(lax.div(t - at, 2), here)
 
+    def begin():
+        def arrange_some(first, last):
+            lax.fori_loop(first, last, arrange, 0)
+
+        def send_first(*ms):
+            for m in ms:
+                for c in ag_copies(m, 0, 0):
+                    c.start()
+        for c in loads:
+            c.start()
+        cx.start()
+        cdy.start()
+        for c in loads:
+            c.wait()
+        arrange_some(0, 2)
+        pl.semaphore_wait(barrier, len(everyone))
+        swap.start()
+        send_first(0, 1)
+        arrange_some(2, UNITS)
+        swap.wait()
+        for l in range(L):
+            for side in BOTH:
+                @pl.when(zh == side)
+                def _():
+                    for b in BOTH:
+                        dbuf[pl.ds(28 * (side ^ b), 28), :H] = quarter[b, l].astype(f32)
+            for j in range(NC):
+                sw[2, l * NC + j] = dbuf[8 * j:8 * j + 8, :H].astype(bf16)
+        own[2].start()
+        send_first(2)
+        arrange_some(UNITS, 2 * UNITS)
+        for c in own[:2]:
+            c.start()
+        cx.wait()
+        tiles(lambda rs: enter(rs, h[rs, :]))
+        ca0.start()
+        for c in own:
+            c.wait()
+        lax.fori_loop(1, G1, lambda t, _: (ag_tick(t), 0)[1], 0)
+
     def rs_region(m, i, p, v, side):
         slot = lax.rem(i, 3)
 
         def some(start, n):
             return rows(start, n) if side is None else rows(start + n // 2 * side, n // 2)
         if p == 2:
-            return zb[m].at[lax.rem(i, 2), v]
+            return zb[m].at[odd_of(i), v]
         if m == 0:
             return ug.at[slot, some(256 * v, 256) if p == 0 else some(256 * mx + 64 * v, 64)]
         if m == 1:
@@ -233,7 +254,7 @@
         return ud.at[slot, some(128 * zp + 32 * v, 32), rows(C * zh, C)]
 
     def rs_landing(m, i, p, k, d):
-        slot = lax.rem(i, 2)
+        slot = odd_of(i)
         if p == 2:
             return r3[m].at[slot, d]
         return halves[p][m].at[slot, d] if k == 1 else fulls[p][m].at[slot, k - 2, d]
@@ -241,7 +262,7 @@
     def rs_copies(m, i, s):
         p, k = rs_stages(m)[s]
         axis = RS_AXES[m][p]
-        slot = lax.rem(i, 2)
+        slot = odd_of(i)
 
         def copy(v, side, d, n, device):
             return remote(rs_region(m, i, p, v, side), rs_landing(m, i, p, k, d), rss.at[slot, m, n], rsr.at[slot, m, n], device)
@@ -262,7 +283,7 @@
         if count == 1:
             tile(0)
         else:
-            lax.fori_loop(0, count, lambda q, _: (tile(q), 0)[1], 0)
+            lax.fori_loop(0, count, lambda q, _: (tile(q), 0)[1], 0, unroll=True)
 
     def rs_stage(m, i, s):
         todo = rs_stages(m)
@@ -273,9 +294,9 @@
             axis = RS_AXES[m][p]
             n = SIZE[axis]
             if p == 2:
-                total = zb[m][lax.rem(i, 2), me[axis]].astype(f32)
+                total = zb[m][odd_of(i), me[axis]].astype(f32)
                 for o in range(n - 1):
-                    total += r3[m][lax.rem(i, 2), o].astype(f32)
+                    total += r3[m][odd_of(i), o].astype(f32)
                 res[m, i] = total.astype(bf16)
             elif k < n // 2:
                 for d, sign in enumerate((1, -1)):
@@ -292,7 +313,7 @@
                         mine[ix] = v.astype(bf16)
                     else:
                         last = SIZE[RS_AXES[m][2]]
-                        zb[m][lax.rem(i, 2)] = v.reshape(last, 8, C).astype(bf16)
+                        zb[m][odd_of(i)] = v.reshape(last, 8, C).astype(bf16)
                 add_tiles(mine, [rs_landing(m, i, p, k, d) for d in BOTH], put)
         if s < len(todo):
             for c in rs_copies(m, i, s):
@@ -302,8 +323,8 @@
         for at in range(PER):
             @pl.when(sub == at)
             def _():
-                for back in range(4, -1, -1):
-                    here = [(m, s) for m in range(3) for s, place in enumerate(PLACE[m]) if place == at + PER * back]
+                for back in range(5)[::1 if at % 2 else -1]:
+                    here = [(m, s) for m in MATRICES for s, place in enumerate(PLACE[m]) if place == at + PER * back]
                     if here:
                         @pl.when((i >= back) & (i < back + UNITS))
                         def _():
@@ -355,7 +376,7 @@
         return wg[slot].reshape(D, C), wu[slot].reshape(D, C)
 
     def gu_copies(n, back):
-        slot = lax.rem(n, 2)
+        slot = odd_of(n)
         j, r = parts(n, NR)
         out = []
         for b, st in enumerate((gst, ust)):
@@ -384,9 +405,12 @@
     def kept_rows(st):
         return [[ref.at[st, q * HT:q * HT + HT] for q in BOTH] for ref in (gst, ust)]
 
-    def late_copies(back):
-        pairs = [(v, late_hbm.at[b]) for b, v in enumerate((dg, du))]
-        return [pltpu.make_async_copy(*(p[::-1] if back else p), lsem.at[b]) for b, p in enumerate(pairs)]
+    def late_buffers(k):
+        return (a.at[:, :C], a.at[:, C:]) if k % 2 else (dg, du)
+
+    def late_copies(k, refs, back):
+        pairs = [(v, late_hbm.at[k - 1, b], lsem.at[odd_of(k), b]) for b, v in enumerate(refs)]
+        return [pltpu.make_async_copy(*((far, v) if back else (v, far)), sem) for v, far, sem in pairs]
 
     def tiles(f):
         lax.fori_loop(0, T // 256, lambda q, _: (f(rows(q * 256, 256)), 0)[1], 0)
@@ -409,28 +433,18 @@
         j1, r1 = parts(g + 1, NR)
         cc = jnp.where(backward, NC + i, j1 - (G1 + 1) // NR)
         r = jnp.where(backward, sub, r1)
-        slot = lax.rem(cc + 2 * NC, 2)
+        slot = odd_of(cc + 2 * NC)
         n1 = g - G1
         rs = rows(lax.rem(r, NR) * TM, TM)
         quarters = [rows(lax.rem(r, NR) * TM + q * HT, HT) for q in BOTH]
 
-        @pl.when((g < G2 - NR) | (backward & (g < 2 * UNITS + G1)))
+        @pl.when((g < G2 - NR) | (backward & (sub < NR) & (i < NC)))
         def _():
-            @pl.when(g == 1)
-            def _():
-                for c in own:
-                    c.wait()
             with jax.named_scope("gather"):
-                ag_tick(jnp.where(backward, g - NR, g))
+                ag_tick(jnp.where(backward, G2 - NR + NR * i + sub, g))
 
         @pl.when(r == 0)
         def _():
-            @pl.when(g == 1)
-            def _():
-                cx.wait()
-                tiles(lambda rs: enter(rs, h[rs, :]))
-                ca0.start()
-
             @pl.when(g == G1 + NR)
             def _():
                 tiles(clear)
@@ -454,7 +468,7 @@
                     tiles(leave)
                 cx.start()
 
-            @pl.when((g < G4) & (cc >= 0))
+            @pl.when(g < G4)
             def _():
                 with jax.named_scope("weights"):
                     @pl.when((cc < NC) | backward)
@@ -469,7 +483,7 @@
                     def _():
                         w_wait(1 - slot, True)
 
-        @pl.when((r == 1) & (cc >= -1) & (cc < 3 * NC))
+        @pl.when((r == 1) & (cc < 3 * NC))
         def _():
             nxt = cc + 1
 
@@ -481,13 +495,13 @@
             def _():
                 w_start(jnp.where(nxt < UNITS, nxt, nxt - UNITS), 1 - slot, True)
 
-            @pl.when((cc >= 0) & (g < G2))
+            @pl.when(g < G2)
             def _():
                 w_start(cc, slot, True)
 
-        @pl.when((n1 >= 0) & (g < G2))
+        @pl.when(g < G2)
         def _():
-            st = lax.rem(n1, 2)
+            st = odd_of(n1)
 
             @pl.when((n1 >= 2) & (n1 < NC * NR))
             def _():
@@ -522,8 +536,9 @@
             def _():
                 with jax.named_scope("row2"):
                     wgs, wus = gate_up(slot)
-                    gst[0] = dot(a[rs, :], wgs)
-                    ust[0] = dot(a[rs, :], wus)
+                    for q, part in enumerate(quarters):
+                        gst[0, q * HT:q * HT + HT] = dot(a[part, :], wgs)
+                        ust[0, q * HT:q * HT + HT] = dot(a[part, :], wus)
                     back_rows(*kept_rows(0), quarters, slot, True)
 
             @pl.when((sub < NR) & (g >= G3) & (g < G4))
@@ -536,16 +551,16 @@
                 def _():
                     for c in gu_copies(n + 1, True):
                         c.start()
-                kept = kept_rows(lax.rem(n, 2))
+                kept = kept_rows(odd_of(n))
 
                 @pl.when(i < UNITS - LATE)
                 def _():
                     with jax.named_scope("row3"):
                         back_rows(*kept, quarters, slot, True)
 
-                @pl.when((i >= UNITS - LATE) & (n == NR * (NC - 1)))
-                def _():
-                    for c in late_copies(False):
+                @pl.when((i > UNITS - LATE) & (sub == 0))
+                def _():
+                    for c in late_copies(UNITS - i, (dg, du), False):
                         c.wait()
 
                 @pl.when(i >= UNITS - LATE)
@@ -559,9 +574,9 @@
                 def _():
                     ca.wait()
 
-                @pl.when(i == UNITS - LATE)
-                def _():
-                    for c in late_copies(False):
+                @pl.when((i >= UNITS - LATE) & (i < UNITS - 1))
+                def _():
+                    for c in late_copies(UNITS - 1 - i, (dg, du), False):
                         c.start()
                 with jax.named_scope("dd"):
                     ud[mine] = dot(act[...], dy[...], 0, 0).astype(bf16)
@@ -576,39 +591,57 @@
             def _():
                 n = g - G4
 
-                @pl.when(n == NR + 1)
-                def _():
-                    for c in late_copies(True):
-                        c.wait()
-
-                @pl.when((n < NR) | ((n > NR) & (n <= 2 * NR)))
-                def _():
-                    late, q = parts(n, NR + 1)
-                    rs = rows(q * TM, TM)
-                    with jax.named_scope("late"):
-                        add_da(rs, dg[rs, :], du[rs, :], late)
-
-                @pl.when(n == NR - 1)
-                def _():
-                    for c in late_copies(True):
+                k, q = parts(n, NR)
+                kslot = odd_of(k)
+
+                @pl.when(n == 0)
+                def _():
+                    for c in late_copies(1, late_buffers(1), True):
                         c.start()
 
-                @pl.when(n == NR)
+                for odd in BOTH:
+                    here = (kslot == odd) & (k < LATE)
+
+                    @pl.when(here & (q == 0) & (k > 0))
+                    def _():
+                        for c in late_copies(k, late_buffers(odd), True):
+                            c.wait()
+
+                        @pl.when(k > 1)
+                        def _():
+                            w_wait(kslot, False)
+
+                    @pl.when(here)
+                    def _():
+                        tile = rows(q * TM, TM)
+                        with jax.named_scope("late"):
+                            add_da(tile, *(ref[tile, :] for ref in late_buffers(odd)), kslot)
+
+                    @pl.when(here & (q == NR - 1) & (k < LATE - 2))
+                    def _():
+                        for c in late_copies(k + 2, late_buffers(odd), True):
+                            c.start()
+                        w_start(NC - 3 - k, kslot, False)
+
+                @pl.when(n == 0)
                 def _():
                     cx.wait()
 
-                @pl.when((n == NR) | (g == GEND - 1))
+                @pl.when(g >= GEND - 2)
                 def _():
                     with jax.named_scope("collect"):
-                        collect(jnp.where(n == NR, 1, 0))
-
-                @pl.when(n == 2 * NR + 1)
+                        collect(GEND - 1 - g)
+
+                @pl.when(g == GEND - 3)
                 def _():
                     tiles(leave)
                     cdx.start()
         return 0
 
-    lax.fori_loop(0, GEND, step, 0)
+    with jax.named_scope("begin"):
+        begin()
+    w_start(0, 0, False)
+    lax.fori_loop(G1, GEND, step, 0)
     ends = [pltpu.make_async_copy(raw.at[0], og_hbm, isem.at[2]), pltpu.make_async_copy(raw.at[1], ou_hbm, isem.at[3]),
             pltpu.make_async_copy(outd, od_hbm, isem.at[4])]
     for c in ends[:2]:
@@ -629,7 +662,7 @@
     hbm = pl.BlockSpec(memory_space=pl.ANY)
     outs = [S((T, D), bf16), S((L, 8, FF), bf16), S((L, 8, FF), bf16), S((L, 28, D), bf16),
             *[S((UNITS, 2, X, H, H), bf16)] * 2, S((UNITS, 2, 2, C, H), bf16),
-            S((T, D), bf16), S((NC, 2, T, C), f32), S((2, T, C), bf16)]
+            S((T, D), bf16), S((NC, 2, T, C), f32), S((LATE - 1, 2, T, C), bf16)]
     scratch = [
         *[V((T, D), bf16)] * 3, V((T, D), f32),
         *[V((2, X, H, C), bf16)] * 2, V((2, C, D), bf16),
@@ -642,7 +675,7 @@
         tuple(V((2, SIZE[axes[2]] - 1, 8, C), bf16) for axes in RS_AXES),
         V((3, UNITS, 8, C), bf16), V((2, L, 8, FF), bf16), V((3, UNITS, 8, H), bf16), V((2, L, 28, H), bf16),
         V((L, 28, D), bf16), V((2, L, 28, C), bf16), V((56, C), f32),
-        DMA((6,)), DMA((2, 3)), DMA((2, 2)), DMA((2,)), *[DMA((AG_SLOTS, 3, SEMS))] * 2, *[DMA((2, 3, SEMS))] * 2,
+        DMA((6,)), DMA((2, 3)), *[DMA((2, 2))] * 2, *[DMA((AG_SLOTS, 3, SEMS))] * 2, *[DMA((2, 3, SEMS))] * 2,
         DMA((2, 3)),
     ]
     return pl.pallas_call(

time: 437 us -> 423 us (0.968)
  Pallas kernels: 426 us -> 411 us
    pallas_call x1, Pallas kernels: 426 us -> 411 us  [mega(): pl.pallas_call(kernel, out_shape=outs, in_specs=[hbm] * 5, out_specs=[hbm...]
    unnamed x9 -> x5, local copies, waits for them, and re-layouts: 9.22 us -> 11 us
where the time goes in v2:
time: 423 us
  Pallas kernels  411 us (97%)
  local copies, waits for them, and re-layouts  11 us (3%)
    pallas_call x1, Pallas kernels, mega(): pl.pallas_call(kernel, out_shape=outs, in_specs=[hbm] * 5, out_specs=[hbm...  411 us
    unnamed x5, local copies, waits for them, and re-layouts  11 us

profile of v2, /device:TPU:64, one launch (start us, length us, event | category | flops | bytes accessed | tf_op | source)
XLA Modules:
  0.0 422.7 jit_solution(12811257938088794879)
XLA Ops:
  0.6 1.6 copy.9.down_hbm
  2.2 411.1 %mega.1 = (bf16[2048,1024]{1,0:T(8,128)(2,1)}, bf16[2,8,3584]{2,1,0:T(8,128)(2,1)}, bf16[2,8,3584]{2,1,0:T(8,128)(2,1)}, bf16[2,28,1024]{2,1,0:T(8,128)(2,1)}, b...) custom-call(bf16[2048,1024]{1,0:T(8,128)(2,1)} %bitcast.3, ...), custom_call_target="tpu_custom_call" | custom-call | tf_op jit(solution)/shard_map/mega/pallas_call | solution.py:681
  413.3 1.7 copy.10
  415.0 4.6 %copy.14 = bf16[1,2048,1024]{2,1,0:T(8,128)(2,1)} copy(bf16[1,2048,1024]{2,1,0:T(8,128)(2,1)} %bitcast.5) | data formatting | bytes 8388608
  419.6 1.6 copy.15
  421.2 1.6 copy.16

commit v3 on v2

--- a/solution.py
+++ b/solution.py
@@ -8,7 +8,7 @@
 T, D, FF, L = 2048, 1024, 3584, 2
 X, Y, Z = 4, 4, 8
 C, NC = 512, 7
-H, LANES = C // 2, 128
+H, LANES, SPAN, EACH = C // 2, 128, 64, 28
 TM = 1024
 HT = TM // 2
 BOTH, MATRICES = range(2), range(3)
@@ -23,7 +23,7 @@
 GU_PLACE = (4, 6, 9, 11, 13, 16)
 PLACE = (GU_PLACE, GU_PLACE, (3, 4, 7, 9, 11, 12, 14, 16))
 GU_TICK = (0, 2, 3, 5, 7, 8)
-TICK = (GU_TICK, GU_TICK, (0, 1, 3, 4, 5, 6, 7, 8))
+TICK = (GU_TICK, GU_TICK, tuple(t for t in range(9) if t != 2))
 G1 = 9
 G2 = G1 + NR * NC + NR
 G3 = G2 + PER * NC
@@ -115,13 +115,13 @@
     loads = [pltpu.make_async_copy(gate_hbm, raw.at[0], isem.at[2]), pltpu.make_async_copy(up_hbm, raw.at[1], isem.at[3]),
              pltpu.make_async_copy(down_hbm.at[:, :, my_columns(zh)], quarter.at[0], isem.at[4])]
     own = [
-        pltpu.make_async_copy(sw.at[0], wg_hbm.at[:, rep, mx, rows(64 * my + 8 * mz, 8)], isem.at[2]),
-        pltpu.make_async_copy(sw.at[1], wu_hbm.at[:, rep, mx, rows(64 * my + 8 * mz, 8)], isem.at[3]),
-        pltpu.make_async_copy(sw.at[2], wd_hbm.at[:, zh, rep, rows(128 * zp + 32 * mx + 8 * my, 8)], isem.at[4]),
+        pltpu.make_async_copy(sw.at[0], wg_hbm.at[:, rep, mx, rows(SPAN * my + 8 * mz, 8)], isem.at[2]),
+        pltpu.make_async_copy(sw.at[1], wu_hbm.at[:, rep, mx, rows(SPAN * my + 8 * mz, 8)], isem.at[3]),
+        pltpu.make_async_copy(sw.at[2], wd_hbm.at[:, zh, rep, rows(LANES * zp + 32 * mx + 8 * my, 8)], isem.at[4]),
     ]
     swap = remote(down_hbm.at[:, :, my_columns(1 - zh)], quarter.at[1], psem.at[0, 0], psem.at[1, 0], twin)
 
-    group = lax.shift_right_logical(lax.broadcasted_iota(jnp.int32, (8, 128), 1), 3)
+    group = lax.shift_right_logical(lax.broadcasted_iota(jnp.int32, (8, LANES), 1), 3)
 
     def arrange(n, _):
         l, q = parts(n, NC * 2)
@@ -142,19 +142,19 @@
             return rows(start, n) if side is None else rows(start + n // 2 * side, n // 2)
         if m == 2:
             if p == 0:
-                return wd_hbm.at[u, zh, rep, rows(128 * zp + 32 * mx + 8 * v, 8)]
+                return wd_hbm.at[u, zh, rep, rows(LANES * zp + 32 * mx + 8 * v, 8)]
             if p == 1:
-                return wd_hbm.at[u, zh, rep, rows(128 * zp + 32 * v, 32)]
+                return wd_hbm.at[u, zh, rep, rows(LANES * zp + 32 * v, 32)]
             pair, odd = parts(v, 2)
-            return wd_hbm.at[u, odd, rep, some(128 * pair, 128)]
+            return wd_hbm.at[u, odd, rep, some(LANES * pair, LANES)]
         w = (wg_hbm, wu_hbm)[m]
         if p == 0:
-            return w.at[u, rep, mx, rows(64 * my + 8 * v, 8)]
+            return w.at[u, rep, mx, rows(SPAN * my + 8 * v, 8)]
         if m == 0:
-            return w.at[u, rep, mx, rows(64 * v, 64)] if p == 1 else w.at[u, rep, v, some(0, 256)]
+            return w.at[u, rep, mx, rows(SPAN * v, SPAN)] if p == 1 else w.at[u, rep, v, some(0, H)]
         if p == 1:
-            return w.at[u, rep, v, rows(64 * my, 64)]
-        return w.at[u, rep, some(0, X), rows(64 * v, 64)]
+            return w.at[u, rep, v, rows(SPAN * my, SPAN)]
+        return w.at[u, rep, some(0, X), rows(SPAN * v, SPAN)]
 
     def ag_copies(m, u, s):
         slot = lax.rem(u, AG_SLOTS)
@@ -222,7 +222,7 @@
                 @pl.when(zh == side)
                 def _():
                     for b in BOTH:
-                        dbuf[pl.ds(28 * (side ^ b), 28), :H] = quarter[b, l].astype(f32)
+                        dbuf[pl.ds(EACH * (side ^ b), EACH), :H] = quarter[b, l].astype(f32)
             for j in range(NC):
                 sw[2, l * NC + j] = dbuf[8 * j:8 * j + 8, :H].astype(bf16)
         own[2].start()
@@ -245,13 +245,13 @@
         if p == 2:
             return zb[m].at[odd_of(i), v]
         if m == 0:
-            return ug.at[slot, some(256 * v, 256) if p == 0 else some(256 * mx + 64 * v, 64)]
+            return ug.at[slot, some(H * v, H) if p == 0 else some(H * mx + SPAN * v, SPAN)]
         if m == 1:
-            return uu.at[slot, some(0, X), rows(64 * v, 64)] if p == 0 else uu.at[slot, v, some(64 * my, 64)]
+            return uu.at[slot, some(0, X), rows(SPAN * v, SPAN)] if p == 0 else uu.at[slot, v, some(SPAN * my, SPAN)]
         if p == 0:
             pair, odd = parts(v, 2)
-            return ud.at[slot, some(128 * pair, 128), rows(C * odd, C)]
-        return ud.at[slot, some(128 * zp + 32 * v, 32), rows(C * zh, C)]
+            return ud.at[slot, some(LANES * pair, LANES), rows(C * odd, C)]
+        return ud.at[slot, some(LANES * zp + 32 * v, 32), rows(C * zh, C)]
 
     def rs_landing(m, i, p, k, d):
         slot = odd_of(i)
@@ -273,7 +273,7 @@
 
     def add_tiles(dst, srcs, put):
         *lead, n, _ = dst.shape
-        t = min(n, 64)
+        t = min(n, SPAN)
         count = (lead[0] if lead else 1) * (n // t)
 
         def tile(q):
@@ -334,6 +334,17 @@
     def send_half(l):
         return remote(half.at[0, l], half.at[1, l], psem.at[0, 1 + l], psem.at[1, 1 + l], twin)
 
+    def collect_down(l):
+        i0 = (L - 1 - l) * NC
+        for j in range(NC):
+            dbuf[8 * j:8 * j + 8, :] = res[2, i0 + j].astype(f32)
+        for side in BOTH:
+            @pl.when(zh == side)
+            def _():
+                half[0, l] = dbuf[EACH - EACH * side:56 - EACH * side, :].astype(bf16)
+                outd[l, :, C * side:C * side + C] = dbuf[EACH * side:EACH * side + EACH, :].astype(bf16)
+        send_half(l).start()
+
     def collect(l):
         i0 = (L - 1 - l) * NC
 
@@ -341,20 +352,12 @@
             for t in range(FF // LANES):
                 out = jnp.zeros((8, LANES), f32)
                 for q in range(X * Y):
-                    xy, w = divmod(16 * t + q, 28)
+                    xy, w = divmod(16 * t + q, EACH)
                     quad, j = divmod(w, NC)
                     lanes = pltpu.roll(res[m, i0 + j, :, LANES * quad:LANES * (quad + 1)].astype(f32), (8 * q - 8 * xy) % LANES, 1)
                     out = jnp.where(group == q, lanes, out)
                 raw[m, l, :, LANES * t:LANES * (t + 1)] = out.astype(bf16)
             return 0
-        for j in range(NC):
-            dbuf[8 * j:8 * j + 8, :] = res[2, i0 + j].astype(f32)
-        for side in BOTH:
-            @pl.when(zh == side)
-            def _():
-                half[0, l] = dbuf[28 - 28 * side:56 - 28 * side, :].astype(bf16)
-                outd[l, :, C * side:C * side + C] = dbuf[28 * side:28 * side + 28, :].astype(bf16)
-        send_half(l).start()
         lax.fori_loop(0, 2, tile, 0)
 
     def w_copies(u, slot, down):
@@ -413,10 +416,10 @@
         return [pltpu.make_async_copy(*((far, v) if back else (v, far)), sem) for v, far, sem in pairs]
 
     def tiles(f):
-        lax.fori_loop(0, T // 256, lambda q, _: (f(rows(q * 256, 256)), 0)[1], 0)
+        lax.fori_loop(0, T // H, lambda q, _: (f(rows(q * H, H)), 0)[1], 0)
 
     def clear(rs):
-        acc[rs, :] = jnp.zeros((256, D), f32)
+        acc[rs, :] = jnp.zeros((H, D), f32)
 
     def enter(rs, new):
         h[rs, :] = new
@@ -630,6 +633,7 @@
                 @pl.when(g >= GEND - 2)
                 def _():
                     with jax.named_scope("collect"):
+                        collect_down(GEND - 1 - g)
                         collect(GEND - 1 - g)
 
                 @pl.when(g == GEND - 3)
@@ -660,7 +664,7 @@
     V = pltpu.VMEM
     DMA = pltpu.SemaphoreType.DMA
     hbm = pl.BlockSpec(memory_space=pl.ANY)
-    outs = [S((T, D), bf16), S((L, 8, FF), bf16), S((L, 8, FF), bf16), S((L, 28, D), bf16),
+    outs = [S((T, D), bf16), S((L, 8, FF), bf16), S((L, 8, FF), bf16), S((L, EACH, D), bf16),
             *[S((UNITS, 2, X, H, H), bf16)] * 2, S((UNITS, 2, 2, C, H), bf16),
             S((T, D), bf16), S((NC, 2, T, C), f32), S((LATE - 1, 2, T, C), bf16)]
     scratch = [
@@ -673,8 +677,8 @@
               for p, shapes in enumerate(HALVES)),
         tuple(V((2, SIZE[axes[2]], 8, C), bf16) for axes in RS_AXES),
         tuple(V((2, SIZE[axes[2]] - 1, 8, C), bf16) for axes in RS_AXES),
-        V((3, UNITS, 8, C), bf16), V((2, L, 8, FF), bf16), V((3, UNITS, 8, H), bf16), V((2, L, 28, H), bf16),
-        V((L, 28, D), bf16), V((2, L, 28, C), bf16), V((56, C), f32),
+        V((3, UNITS, 8, C), bf16), V((2, L, 8, FF), bf16), V((3, UNITS, 8, H), bf16), V((2, L, EACH, H), bf16),
+        V((L, EACH, D), bf16), V((2, L, EACH, C), bf16), V((56, C), f32),
         DMA((6,)), DMA((2, 3)), *[DMA((2, 2))] * 2, *[DMA((AG_SLOTS, 3, SEMS))] * 2, *[DMA((2, 3, SEMS))] * 2,
         DMA((2, 3)),
     ]
@@ -684,9 +688,33 @@
     )(x, dy, gate, up, down)[:4]
 
 
+def hand_over(*arrays):
+    k, n = len(arrays), 8
+
+    def move(*refs):
+        ins, outs, kept, sems = refs[:k], refs[k:-k - 1], refs[-k - 1:-1], refs[-1]
+        first, *others = zip(ins, kept, outs)
+        steps = [[ref.at[pl.ds(q * T // n, T // n)] for ref in first] for q in range(n)] + others
+        reads, writes = ([pltpu.make_async_copy(*step[b:b + 2], sems.at[b, q]) for q, step in enumerate(steps)] for b in BOTH)
+        for c in reads:
+            c.start()
+        for c, d in zip(reads, writes):
+            c.wait()
+            d.start()
+        for d in writes:
+            d.wait()
+    hbm = [pl.BlockSpec(memory_space=pl.ANY)] * k
+    like = [jax.ShapeDtypeStruct(t.shape, t.dtype) for t in arrays]
+    return pl.pallas_call(
+        move, out_shape=like, in_specs=hbm, out_specs=hbm, name="hand_over",
+        scratch_shapes=[pltpu.VMEM(t.shape, t.dtype) for t in like] + [pltpu.SemaphoreType.DMA((2, n + k))],
+    )(*arrays)
+
+
 def body(x, dy, *weights):
-    dx, *by_weights = mega(x[0], dy[0], *weights)
-    return (dx[None], *by_weights)
+    dx, gate, up, down = mega(x[0], dy[0], *weights)
+    dx, gate, up = hand_over(dx, gate, up)
+    return dx[None], gate, up, down
 
 
 def solution(mesh):

time: 423 us -> 419 us (level)
  local copies, waits for them, and re-layouts: 11 us -> 3.24 us
    unnamed x5 -> x2, local copies, waits for them, and re-layouts: 11 us -> 3.24 us
where the time goes in v3:
time: 419 us
  Pallas kernels  415 us (99%)
    pallas_call x1, Pallas kernels, mega(): pl.pallas_call(kernel, out_shape=outs, in_specs=[hbm] * 5, out_specs=[hbm...  411 us

profile of v3, /device:TPU:64, one launch (start us, length us, event | category | flops | bytes accessed | tf_op | source)
XLA Modules:
  0.0 418.9 jit_solution(17150175215971636767)
XLA Ops:
  0.6 1.6 copy.9.down_hbm
  2.2 411.3 %mega.1 = (bf16[2048,1024]{1,0:T(8,128)(2,1)}, bf16[2,8,3584]{2,1,0:T(8,128)(2,1)}, bf16[2,8,3584]{2,1,0:T(8,128)(2,1)}, bf16[2,28,1024]{2,1,0:T(8,128)(2,1)}, b...) custom-call(bf16[2048,1024]{1,0:T(8,128)(2,1)} %bitcast.3, ...), custom_call_target="tpu_custom_call" | custom-call | tf_op jit(solution)/shard_map/mega/pallas_call | solution.py:685
  413.5 3.7 hand_over.1
  417.2 1.7 copy.10
